TPU v7x, 32 devices: a whole 2x2x4 slice. The times are simulated.
32 devices in a mesh: group: 2 (over y), expert: 8 (over z, x), tensor: 2 (over core).
Axes of the slice: x: 2, y: 2, z: 4, core: 2. Of those that a mesh axis runs over, the one named last changes fastest.
Arguments:
- tokens: bfloat16 [16, 256, 1280], P(('group', 'expert'), 'tensor'), parts along dimension 0, may hold values from -6 to 6
- ln_gain: float32 [1280], replicated, may hold values from 0.5 to 1.5
- slot_keys: bfloat16 [1280, 8], P(None, 'expert'), may hold values from -0.3125 to 0.3125
- w_gate: bfloat16 [8, 1280, 1280], P('expert', 'tensor'), may hold values from -0.15625 to 0.15625
- w_up: bfloat16 [8, 1280, 1280], P('expert', 'tensor'), may hold values from -0.15625 to 0.15625
- w_down: bfloat16 [8, 1280, 1280], P('expert', 'tensor'), may hold values from -0.25 to 0.25
Outputs:
- output: bfloat16 [16, 256, 1280], P(('group', 'expert'), 'tensor'), parts along dimension 0
There are 2 independent parts, one for each index of `group`. A program takes and returns all parts, laid end to end along the dimension named above; an argument that names none is the same for every part. Nothing has to cross between parts.
All inputs are finite; a program needn't handle non-finite values.
Results may differ from a plain program's by a relative error of at most 0.0034.
Values may be sent and summed in bfloat16 or wider, within the bound.
A program may use at most 64 MiB of HBM per device.

v0:
```python
import functools

import jax
import jax.numpy as jnp
from jax import lax
from jax.experimental import pallas as pl
from jax.experimental.pallas import tpu as pltpu
from jax.sharding import PartitionSpec as P

epsilon = 1e-06
soft_cap = 20.0
MESH = pl.DeviceIdType.MESH
f32 = jnp.float32
bf16 = jnp.bfloat16


def repeat(count, body):
    if count <= 16:
        for k in range(count):
            body(k)
    else:
        lax.fori_loop(0, count, lambda k, c: (body(k), c)[1], 0)


def layer_kernel(
    n, tokens_hbm, gain_hbm, key_hbm, gate_hbm, up_hbm, down_hbm, out_ref,
    tok, gain_ref, key_ref, gate_w, up_w, down_w, normed, turned, keys, slot_send, arrived, rows,
    part, part_theirs, out_send, back, load_sem, key_sem, row_sem, back_sem, pair_sem,
):
    me = lax.axis_index("expert")
    core = lax.axis_index("tensor")
    half, width = tok.shape

    loads = [
        pltpu.make_async_copy(tokens_hbm.at[0], tok, load_sem.at[0]),
        pltpu.make_async_copy(gain_hbm, gain_ref, load_sem.at[1]),
        pltpu.make_async_copy(key_hbm, key_ref, load_sem.at[2]),
        pltpu.make_async_copy(gate_hbm.at[0], gate_w, load_sem.at[3]),
        pltpu.make_async_copy(up_hbm.at[0], up_w, load_sem.at[4]),
        pltpu.make_async_copy(down_hbm.at[0], down_w, load_sem.at[5]),
    ]

    barrier = pltpu.get_barrier_semaphore()

    def peer(k):
        return lax.rem(me + k + 1, n)

    def greet(k):
        pl.semaphore_signal(barrier, inc=1, device_id={"expert": peer(k), "tensor": 1 - core}, device_id_type=MESH)

    repeat(n - 1, greet)
    pl.semaphore_signal(barrier, inc=1, device_id={"tensor": 1 - core}, device_id_type=MESH)
    for load in loads:
        load.start()

    loads[2].wait()
    pl.semaphore_wait(barrier, n)

    def exchange(src_of, dst, sems):
        def start(k):
            pltpu.make_async_remote_copy(
                src_ref=src_of(peer(k)), dst_ref=dst.at[me],
                send_sem=sems.at[0, peer(k)], recv_sem=sems.at[1, me],
                device_id={"expert": peer(k), "tensor": 1 - core}, device_id_type=MESH,
            ).start()

        repeat(n - 1, start)

    def await_arrivals(src_of, dst, sems):
        def wait(k):
            pltpu.make_async_remote_copy(
                src_ref=src_of(peer(k)), dst_ref=dst.at[peer(k)],
                send_sem=sems.at[0, peer(k)], recv_sem=sems.at[1, peer(k)],
                device_id={"expert": peer(k), "tensor": 1 - core}, device_id_type=MESH,
            ).wait_recv()

        repeat(n - 1, wait)

    def await_sends(src_of, dst, sems):
        def wait(k):
            pltpu.make_async_remote_copy(
                src_ref=src_of(peer(k)), dst_ref=dst.at[me],
                send_sem=sems.at[0, peer(k)], recv_sem=sems.at[1, me],
                device_id={"expert": peer(k), "tensor": 1 - core}, device_id_type=MESH,
            ).wait_send()

        repeat(n - 1, wait)

    def pair_copy(src, dst, which):
        return pltpu.make_async_remote_copy(
            src_ref=src, dst_ref=dst,
            send_sem=pair_sem.at[0, which], recv_sem=pair_sem.at[1, which],
            device_id={"tensor": 1 - core}, device_id_type=MESH,
        )

    key_of = lambda j: key_ref
    first = pair_copy(normed.at[core], normed.at[core], 0)
    exchange(key_of, keys, key_sem)
    loads[0].wait()
    widened = tok[...].astype(f32)
    center = widened - jnp.mean(widened, axis=-1, keepdims=True)
    variance = jnp.mean(center * center, axis=-1, keepdims=True)
    loads[1].wait()
    gain = gain_ref[...].reshape(1, width)
    normed[core] = (center * lax.rsqrt(variance + epsilon) * gain).astype(bf16)
    first.start()
    keys[me] = key_ref[...]
    pair_copy(normed.at[1 - core], normed.at[1 - core], 0).wait_recv()
    turned[...] = normed[...].reshape(2 * half, width).T
    await_arrivals(key_of, keys, key_sem)
    all_keys = keys[...].astype(f32).reshape(n, width).astype(bf16)
    image = normed[...].reshape(2 * half, width)
    raw = lax.dot_general(
        all_keys, turned[...], (((1,), (0,)), ((), ())), preferred_element_type=f32
    )
    scores = jnp.exp(soft_cap * jnp.tanh(raw / soft_cap))
    slot_num = jnp.dot(scores.astype(bf16), image, preferred_element_type=f32)
    slot_in = slot_num / jnp.sum(scores, axis=1, keepdims=True)
    for e in range(n // 2):
        slot_send[e] = slot_in[2 * e:2 * e + 2].astype(bf16)

    slot_of = lambda j: slot_send.at[j // 2]
    exchange(slot_of, arrived, row_sem)
    arrived[me] = slot_send[me // 2]
    own = jnp.where(core == 0, scores[:, :half], scores[:, half:])
    combine = (own / jnp.sum(own, axis=0, keepdims=True)).astype(bf16)
    for load in loads[3:]:
        load.wait()
    await_arrivals(slot_of, arrived, row_sem)
    for g in range(0, n, 8):
        rows[2 * g:2 * g + 16] = jnp.concatenate(
            [arrived[i].astype(f32) for i in range(g, g + 8)], axis=0
        ).astype(bf16)

    contract = (((1,), (1,)), ((), ()))
    gate_act = lax.dot_general(rows[...], gate_w[...], contract, preferred_element_type=f32)
    up_proj = lax.dot_general(rows[...], up_w[...], contract, preferred_element_type=f32)
    hidden = (jax.nn.silu(gate_act) * up_proj).astype(bf16)
    part[...] = jnp.dot(hidden, down_w[...], preferred_element_type=f32)
    second = pair_copy(part, part_theirs, 1)
    second.start()
    second.wait()
    for i in range(n):
        out_send[i] = (part[2 * i:2 * i + 2] + part_theirs[2 * i:2 * i + 2]).astype(bf16)

    out_of = lambda j: out_send.at[j]
    exchange(out_of, back, back_sem)
    back[me] = out_send[me]
    await_arrivals(out_of, back, back_sem)
    slot_out = jnp.concatenate(
        [back[2 * e].astype(f32) + back[2 * e + 1].astype(f32) for e in range(n // 2)], axis=0
    ).astype(bf16)
    mixed = lax.dot_general(
        combine, slot_out, (((0,), (0,)), ((), ())), preferred_element_type=f32
    )
    out_ref[...] = (tok[...].astype(f32) + mixed).astype(bf16)

    first.wait_send()
    await_sends(key_of, keys, key_sem)
    await_sends(slot_of, arrived, row_sem)
    await_sends(out_of, back, back_sem)


def on_device(tokens, ln_gain, slot_keys, w_gate, w_up, w_down):
    n = lax.axis_size("expert")
    _, half, width = tokens.shape
    units = w_gate.shape[1]
    key_row = slot_keys.reshape(1, width)
    vmem = pl.BlockSpec(memory_space=pltpu.VMEM)
    hbm = pl.BlockSpec(memory_space=pl.ANY)
    out = pl.pallas_call(
        functools.partial(layer_kernel, n),
        out_shape=pltpu.VMEM((half, width), bf16),
        in_specs=[hbm] * 6,
        out_specs=vmem,
        scratch_shapes=[
            pltpu.VMEM((half, width), bf16),
            pltpu.VMEM((width,), f32),
            pltpu.VMEM((1, width), bf16),
            pltpu.VMEM((units, width), bf16),
            pltpu.VMEM((units, width), bf16),
            pltpu.VMEM((units, width), bf16),
            pltpu.VMEM((2, half, width), bf16),
            pltpu.VMEM((width, 2 * half), bf16),
            pltpu.VMEM((n, 1, width), bf16),
            pltpu.VMEM((n // 2, 2, width), bf16),
            pltpu.VMEM((n, 2, width), bf16),
            pltpu.VMEM((2 * n, width), bf16),
            pltpu.VMEM((2 * n, width), f32),
            pltpu.VMEM((2 * n, width), f32),
            pltpu.VMEM((n, 2, width), bf16),
            pltpu.VMEM((n, 2, width), bf16),
            pltpu.SemaphoreType.DMA((6,)),
            pltpu.SemaphoreType.DMA((2, n)),
            pltpu.SemaphoreType.DMA((2, n)),
            pltpu.SemaphoreType.DMA((2, n)),
            pltpu.SemaphoreType.DMA((2, 2)),
        ],
        compiler_params=pltpu.CompilerParams(collective_id=0, has_side_effects=True),
    )(tokens, ln_gain, key_row, w_gate, w_up, w_down)
    return out[None]


def solution(mesh):
    placed = (
        P(("group", "expert"), "tensor", None),
        P(),
        P(None, "expert"),
        P("expert", "tensor", None),
        P("expert", "tensor", None),
        P("expert", "tensor", None),
    )
    return jax.shard_map(
        on_device,
        mesh=mesh,
        in_specs=placed,
        out_specs=P(("group", "expert"), "tensor", None),
        check_vma=False,
    )
```

profile of v0, /device:TPU:0, one launch (start us, length us, event | category | flops | bytes accessed | tf_op | source)
XLA Modules:
  0.0 20.0 jit_solution(10966636426675024669)
XLA Ops:
  0.0 19.3 %shard_map.64 = bf16[128,1280]{1,0:T(8,128)(2,1)S(1)} custom-call(bf16[1,128,1280]{2,1,0:T(8,128)(2,1)} %tokens_hbm.1, f32[1280]{0:T(1024)} %gain_hbm.1, bf16[1,1280]{1,0:T(2,128)(2,1)} %bitcast.3, bf16[1,640,1280]{2,1,0:T(8,128)(2,1)} %gate_hbm.1, bf16[1,640,1280]{2,1,0:T(8,128)(2,1)} %up_hbm.1, bf16[1,640,1280]{2,1,0:T(8,128)(2,1)} %down_hbm.1), custom_call_target="tpu_custom_call" | custom-call | tf_op jit(solution)/shard_map/pallas_call | solution.py:171
  19.3 0.7 %copy.8 = bf16[1,128,1280]{2,1,0:T(8,128)(2,1)} copy(bf16[1,128,1280]{2,1,0:T(8,128)(2,1)S(1)} %bitcast.2) | data formatting | bytes 655360
where the time goes:
time: 20.2 us; the launch traced here: 20 us
  Pallas kernels  19.3 us (96%)
  local copies, waits for them, and re-layouts  0.73 us (4%)
    pallas_call x1, Pallas kernels, on_device(): pl.pallas_call(functools.partial(layer_kernel, n), out_shape=pltpu.VMEM((...  19.3 us
    unnamed x1, local copies, waits for them, and re-layouts  0.73 us

commit v1 on v0

v1 whole, which is shorter than its diff:
```python
import functools

import jax
import jax.numpy as jnp
from jax import lax
from jax.experimental import pallas as pl
from jax.experimental.pallas import tpu as pltpu
from jax.sharding import PartitionSpec as P

epsilon = 1e-06
soft_cap = 20.0
MESH = pl.DeviceIdType.MESH
f32 = jnp.float32
bf16 = jnp.bfloat16


def repeat(count, body):
    if count <= 16:
        for k in range(count):
            body(k)
    else:
        lax.fori_loop(0, count, lambda k, c: (body(k), c)[1], 0)


def farthest_first(me, n):
    if n & (n - 1):
        return lambda k: lax.rem(me + n - 1 - k, n)

    def peer(k):
        mask, out, bit = n - 1 - k, 0, 1
        while bit < n:
            out = out + ((me // bit + mask // bit) % 2) * bit
            bit *= 2
        return out

    return peer


def layer_kernel(
    n, tokens_hbm, gain_hbm, key_hbm, gate_hbm, up_hbm, down_hbm, out_ref,
    tok, gain_ref, key_ref, gate_w, up_w, down_w, gate_t, up_t, normed, turned, keys, slot_send, arrived, rows,
    out_send, back, load_sem, send_sem, recv_sem, pair_sem,
):
    me = lax.axis_index("expert")
    core = lax.axis_index("tensor")
    half, width = tok.shape
    peer = farthest_first(me, n)

    loads = [
        pltpu.make_async_copy(key_hbm, key_ref, load_sem.at[0]),
        pltpu.make_async_copy(tokens_hbm.at[0], tok, load_sem.at[1]),
        pltpu.make_async_copy(gain_hbm, gain_ref, load_sem.at[2]),
        pltpu.make_async_copy(gate_hbm.at[0], gate_w, load_sem.at[3]),
        pltpu.make_async_copy(up_hbm.at[0], up_w, load_sem.at[4]),
        pltpu.make_async_copy(down_hbm.at[0], down_w, load_sem.at[5]),
    ]
    barrier = pltpu.get_barrier_semaphore()

    def greet(k):
        for c in range(2):
            pl.semaphore_signal(barrier, inc=1, device_id={"expert": peer(k), "tensor": c}, device_id_type=MESH)

    repeat(n - 1, greet)
    pl.semaphore_signal(barrier, inc=1, device_id={"tensor": 1 - core}, device_id_type=MESH)
    for load in loads:
        load.start()
    loads[0].wait()
    pl.semaphore_wait(barrier, 2 * n - 1)

    def send(src, dst, phase, where):
        return pltpu.make_async_remote_copy(
            src_ref=src, dst_ref=dst, send_sem=send_sem.at[phase], recv_sem=recv_sem.at[phase],
            device_id=where, device_id_type=MESH,
        )

    def drain(sems, phase, ref, count):
        whole = ref.at[pl.ds(0, count)]
        pltpu.make_async_copy(whole, whole, sems.at[phase]).wait()

    def pair_copy(which):
        return pltpu.make_async_remote_copy(
            src_ref=normed.at[which], dst_ref=normed.at[which],
            send_sem=pair_sem.at[0], recv_sem=pair_sem.at[1],
            device_id={"tensor": 1 - core}, device_id_type=MESH,
        )

    repeat(n - 1, lambda k: send(key_ref, keys.at[me], 0, {"expert": peer(k), "tensor": 1 - core}).start())
    loads[1].wait()
    widened = tok[...].astype(f32)
    center = widened - jnp.mean(widened, axis=-1, keepdims=True)
    variance = jnp.mean(center * center, axis=-1, keepdims=True)
    loads[2].wait()
    gain = gain_ref[...].reshape(1, width)
    normed[core] = (center * lax.rsqrt(variance + epsilon) * gain).astype(bf16)
    pair_copy(core).start()
    keys[me] = key_ref[...]
    pair_copy(1 - core).wait_recv()
    turned[...] = normed[...].reshape(2 * half, width).T
    drain(recv_sem, 0, keys, n - 1)
    all_keys = keys[...].astype(f32).reshape(n, width).astype(bf16)
    image = normed[...].reshape(2 * half, width)
    raw = lax.dot_general(
        all_keys, turned[...], (((1,), (0,)), ((), ())), preferred_element_type=f32
    )
    scores = jnp.exp(soft_cap * jnp.tanh(raw / soft_cap))
    slot_num = jnp.dot(scores.astype(bf16), image, preferred_element_type=f32)
    slot_in = slot_num / jnp.sum(scores, axis=1, keepdims=True)
    for e in range(n // 2):
        slot_send[e] = slot_in[2 * e:2 * e + 2].astype(bf16)

    def send_slots(k):
        send(slot_send.at[peer(k) // 2], arrived.at[me], 1, {"expert": peer(k), "tensor": 1 - core}).start()

    repeat(n - 1, send_slots)
    arrived[me] = slot_send[me // 2]
    own = jnp.where(core == 0, scores[:, :half], scores[:, half:])
    combine = (own / jnp.sum(own, axis=0, keepdims=True)).astype(bf16)
    loads[3].wait()
    gate_t[...] = gate_w[...].T
    loads[4].wait()
    up_t[...] = up_w[...].T
    loads[5].wait()
    drain(recv_sem, 1, arrived, n - 1)
    for g in range(0, n, 8):
        rows[2 * g:2 * g + 16] = jnp.concatenate(
            [arrived[i].astype(f32) for i in range(g, g + 8)], axis=0
        ).astype(bf16)

    gate_act = jnp.dot(rows[...], gate_t[...], preferred_element_type=f32)
    up_proj = jnp.dot(rows[...], up_t[...], preferred_element_type=f32)
    hidden = (jax.nn.silu(gate_act) * up_proj).astype(bf16)
    part = jnp.dot(hidden, down_w[...], preferred_element_type=f32)
    for i in range(n):
        out_send[i] = part[2 * i:2 * i + 2].astype(bf16)

    mine = 2 * me + core

    def send_out(k):
        for c in range(2):
            send(out_send.at[peer(k)], back.at[mine], 2, {"expert": peer(k), "tensor": c}).start()

    repeat(n - 1, send_out)
    send(out_send.at[me], back.at[mine], 2, {"tensor": 1 - core}).start()
    back[mine] = out_send[me]
    drain(recv_sem, 2, back, 2 * n - 1)
    slot_out = jnp.concatenate(
        [sum(back[4 * e + j].astype(f32) for j in range(4)) for e in range(n // 2)], axis=0
    ).astype(bf16)
    mixed = lax.dot_general(
        combine, slot_out, (((0,), (0,)), ((), ())), preferred_element_type=f32
    )
    out_ref[...] = (tok[...].astype(f32) + mixed).astype(bf16)

    pair_copy(core).wait_send()
    drain(send_sem, 0, keys, n - 1)
    drain(send_sem, 1, arrived, n - 1)
    drain(send_sem, 2, back, 2 * n - 1)


def on_device(tokens, ln_gain, slot_keys, w_gate, w_up, w_down):
    n = lax.axis_size("expert")
    _, half, width = tokens.shape
    units = w_gate.shape[1]
    key_row = slot_keys.reshape(1, width)
    vmem = pl.BlockSpec(memory_space=pltpu.VMEM)
    hbm = pl.BlockSpec(memory_space=pl.ANY)
    out = pl.pallas_call(
        functools.partial(layer_kernel, n),
        out_shape=pltpu.VMEM((half, width), bf16),
        in_specs=[hbm] * 6,
        out_specs=vmem,
        scratch_shapes=[
            pltpu.VMEM((half, width), bf16),
            pltpu.VMEM((width,), f32),
            pltpu.VMEM((1, width), bf16),
            pltpu.VMEM((units, width), bf16),
            pltpu.VMEM((units, width), bf16),
            pltpu.VMEM((units, width), bf16),
            pltpu.VMEM((width, units), bf16),
            pltpu.VMEM((width, units), bf16),
            pltpu.VMEM((2, half, width), bf16),
            pltpu.VMEM((width, 2 * half), bf16),
            pltpu.VMEM((n, 1, width), bf16),
            pltpu.VMEM((n // 2, 2, width), bf16),
            pltpu.VMEM((n, 2, width), bf16),
            pltpu.VMEM((2 * n, width), bf16),
            pltpu.VMEM((n, 2, width), bf16),
            pltpu.VMEM((2 * n, 2, width), bf16),
            pltpu.SemaphoreType.DMA((6,)),
            pltpu.SemaphoreType.DMA((3,)),
            pltpu.SemaphoreType.DMA((3,)),
            pltpu.SemaphoreType.DMA((2,)),
        ],
        compiler_params=pltpu.CompilerParams(collective_id=0, has_side_effects=True),
    )(tokens, ln_gain, key_row, w_gate, w_up, w_down)
    return out[None]


def solution(mesh):
    placed = (
        P(("group", "expert"), "tensor", None),
        P(),
        P(None, "expert"),
        P("expert", "tensor", None),
        P("expert", "tensor", None),
        P("expert", "tensor", None),
    )
    return jax.shard_map(
        on_device,
        mesh=mesh,
        in_specs=placed,
        out_specs=P(("group", "expert"), "tensor", None),
        check_vma=False,
    )
```

time: 20.2 us -> 19.2 us (0.950)
  Pallas kernels: 19.3 us -> 18.3 us
    pallas_call x1, Pallas kernels: 19.3 us -> 18.3 us  [on_device(): pl.pallas_call(functools.partial(layer_kernel, n), out_shape=pltpu.VMEM((...]
where the time goes in v1:
time: 19.2 us; the launch traced here: 19.1 us
  Pallas kernels  18.3 us (95%)
  local copies, waits for them, and re-layouts  0.73 us (4%)
    pallas_call x1, Pallas kernels, on_device(): pl.pallas_call(functools.partial(layer_kernel, n), out_shape=pltpu.VMEM((...  18.3 us
    unnamed x1, local copies, waits for them, and re-layouts  0.73 us

profile of v1, /device:TPU:0, one launch (start us, length us, event | category | flops | bytes accessed | tf_op | source)
XLA Modules:
  0.0 19.1 jit_solution(10183126932135372569)
XLA Ops:
  0.0 18.3 %shard_map.64 = bf16[128,1280]{1,0:T(8,128)(2,1)S(1)} custom-call(bf16[1,128,1280]{2,1,0:T(8,128)(2,1)} %tokens_hbm.1, f32[1280]{0:T(1024)} %gain_hbm.1, bf16[1,1280]{1,0:T(2,128)(2,1)} %bitcast.3, bf16[1,640,1280]{2,1,0:T(8,128)(2,1)} %gate_hbm.1, bf16[1,640,1280]{2,1,0:T(8,128)(2,1)} %up_hbm.1, bf16[1,640,1280]{2,1,0:T(8,128)(2,1)} %down_hbm.1), custom_call_target="tpu_custom_call" | custom-call | tf_op jit(solution)/shard_map/pallas_call | solution.py:167
  18.3 0.7 %copy.8 = bf16[1,128,1280]{2,1,0:T(8,128)(2,1)} copy(bf16[1,128,1280]{2,1,0:T(8,128)(2,1)S(1)} %bitcast.2) | data formatting | bytes 655360
